TPU v7x, 32 devices: a whole 2x2x4 slice. The times are simulated.
32 devices in a mesh: rep: 1, dp: 32 (over x, y, z, core).
Axes of the slice: x: 2, y: 2, z: 4, core: 2. Of those that a mesh axis runs over, the one named last changes fastest.
Arguments:
- g_w_gate: bfloat16 [32, 2, 1024, 3200], P(('rep', 'dp'))
- g_w_up: bfloat16 [32, 2, 1024, 3200], P(('rep', 'dp'))
- g_w_down: bfloat16 [32, 2, 3200, 1024], P(('rep', 'dp'))
- w_gate: bfloat16 [2, 1024, 3200], replicated
- w_up: bfloat16 [2, 1024, 3200], replicated
- w_down: bfloat16 [2, 3200, 1024], replicated
- m_w_gate: float32 [2, 1024, 3200], P(None, 'dp')
- m_w_up: float32 [2, 1024, 3200], P(None, 'dp')
- m_w_down: float32 [2, 3200, 1024], P(None, 'dp')
- v_w_gate: float32 [2, 1024, 3200], P(None, 'dp')
- v_w_up: float32 [2, 1024, 3200], P(None, 'dp')
- v_w_down: float32 [2, 3200, 1024], P(None, 'dp')
Outputs:
- output 1: bfloat16 [2, 1024, 3200], P('rep')
- output 2: bfloat16 [2, 1024, 3200], P('rep')
- output 3: bfloat16 [2, 3200, 1024], P('rep')
- output 4: float32 [2, 1024, 3200], P('rep', 'dp')
- output 5: float32 [2, 1024, 3200], P('rep', 'dp')
- output 6: float32 [2, 3200, 1024], P('rep', 'dp')
- output 7: float32 [2, 1024, 3200], P('rep', 'dp')
- output 8: float32 [2, 1024, 3200], P('rep', 'dp')
- output 9: float32 [2, 3200, 1024], P('rep', 'dp')
All inputs are finite; a program needn't handle non-finite values.
Results may differ from a plain program's by a relative error of at most 0.022.
Values are sent between devices in bfloat16 or wider.
A program may use at most 2 GiB of HBM per device.

v0:
```python
import jax
import jax.numpy as jnp
from jax import lax
from jax.sharding import PartitionSpec as P


def adamw(w, m, v, g):
    m = 0.9 * m + 0.1 * g
    v = 0.95 * v + 0.05 * g * g
    step = m * lax.rsqrt(v + 1e-8) + 0.1 * w
    return (w - 0.02 * step).astype(jnp.bfloat16), m, v


def clipped(gradients, sum_of_squares, count):
    factor = jnp.minimum(1.0, 0.5 * lax.rsqrt(sum_of_squares / count + 1e-30))
    return [g * factor for g in gradients]


def solution(mesh):
    def step(*arrays):
        terms, weights, m, v = (arrays[i : i + 3] for i in (0, 3, 6, 9))
        gradients = [lax.psum_scatter(t[0], "dp", scatter_dimension=1, tiled=True).astype(jnp.float32) for t in terms]
        squares = lax.psum(sum(jnp.sum(g * g) for g in gradients), "dp")
        gradients = clipped(gradients, squares, lax.psum(1, "dp") * sum(g.size for g in gradients))
        me = lax.axis_index("dp")
        own = [lax.dynamic_slice_in_dim(w, me * one.shape[1], one.shape[1], 1).astype(jnp.float32) for w, one in zip(weights, m, strict=True)]
        new = [adamw(w, m, v, g) for w, m, v, g in zip(own, m, v, gradients, strict=True)]
        whole = [lax.all_gather(one[0], "dp", axis=1, tiled=True) for one in new]
        return (*whole, *(one[1] for one in new), *(one[2] for one in new))

    all_of, cut = P(None, None, None), P(None, "dp", None)
    return jax.shard_map(
        step,
        mesh=mesh,
        in_specs=(P(("rep", "dp"), None, None, None),) * 3 + (all_of,) * 3 + (cut,) * 6,
        out_specs=(P("rep", None, None),) * 3 + (P("rep", "dp", None),) * 6,
        check_vma=False,
    )
```

profile of v0, /device:TPU:0, one launch (start us, length us, event | category | flops | bytes accessed | tf_op | source)
XLA Modules:
  0.0 972.9 jit_solution(17331262265547800470)
XLA Ops:
  7.2 0.0 all-reduce.3.cloned.1.call-start
  7.2 24.6 %copy.30 = bf16[1,2,3200,1024]{3,1,2,0:T(2,128)(2,1)} copy(bf16[1,2,3200,1024]{3,2,1,0:T(8,128)(2,1)} %param.14) | data formatting | bytes 26214400 | tf_op args[2]
  31.8 0.0 all-reduce.3.cloned.1.call-update
  31.8 0.0 reduce-scatter.3.cloned.1.call-start
  31.9 0.0 copy-start.1
  31.9 0.7 reduce-scatter.3.cloned.1.call-update
  32.6 0.0 reduce-scatter.5.cloned.1.call-start
  32.6 0.7 reduce-scatter.5.cloned.1.call-update
  33.3 0.0 all-gather.8.cloned.1.call-start
  33.4 236.4 %all-reduce.3.cloned.1.call-done = bf16[2,3200,1024]{2,0,1:T(2,128)(2,1)} async-done(((bf16[2,3200,1024]{2,0,1:T(2,128)(2,1)}), bf16[2,3200,1024]{2,0,1:T(2,128)(2,1)}) %all-reduce.3.cloned.1.call-update) | async-done | bytes 13107216
  269.8 2.4 fusion.11
  272.3 164.6 %reduce-scatter.3.cloned.1.call-done = bf16[2,32,3200]{2,1,0:T(8,128)(2,1)} async-done(((bf16[2,1024,3200]{2,1,0:T(8,128)(2,1)}), bf16[2,32,3200]{2,1,0:T(8,128)(2,1)}) %reduce-scatter.3.cloned.1.call-update) | async-done | bytes 409616 | tf_op jit(solution)/shard_map/reduce_scatter | solution.py:22
  436.8 1.8 fusion.9
  438.7 162.8 %reduce-scatter.5.cloned.1.call-done = bf16[2,32,3200]{2,1,0:T(8,128)(2,1)} async-done(((bf16[2,1024,3200]{2,1,0:T(8,128)(2,1)}), bf16[2,32,3200]{2,1,0:T(8,128)(2,1)}) %reduce-scatter.5.cloned.1.call-update) | async-done | bytes 409616 | tf_op jit(solution)/shard_map/reduce_scatter | solution.py:22
  601.5 1.8 fusion.10
  605.2 1.1 constant_dynamic-slice_fusion
  606.4 36.9 %psum.7 = f32[]{:T(128)} all-reduce(f32[]{:T(128)S(6)} %add.65), channel_id=1, replica_groups=mesh['rep'=1,'dp'=32] {'dp'}, use_global_device_ids=true, to_apply=%region_6.0 | all-reduce | flops 1 | bytes 8 | tf_op jit(solution)/shard_map/psum | solution.py:23
  644.0 5.0 fusion.20
  649.0 0.0 all-gather.8.cloned.1.call-update
  649.1 0.0 all-gather.4.cloned.1.call-start
  649.1 2.9 fusion.8
  652.0 0.0 all-gather.4.cloned.1.call-update
  652.1 0.0 all-gather.6.cloned.1.call-start
  652.1 3.2 fusion.14
  655.3 0.0 all-gather.6.cloned.1.call-update
  655.3 93.1 %all-gather.8.cloned.1.call-done = bf16[2,3200,1024]{2,0,1:T(2,128)(2,1)} async-done(((bf16[2,100,1024]{2,0,1:T(2,128)(2,1)}), bf16[2,3200,1024]{2,0,1:T(2,128)(2,1)}) %all-gather.8.cloned.1.call-update) | async-done | bytes 13107216 | tf_op jit(solution)/shard_map/all_gather | solution.py:28
  748.4 12.9 %copy.26 = bf16[2,3200,1024]{2,1,0:T(8,128)(2,1)} copy(bf16[2,3200,1024]{2,0,1:T(2,128)(2,1)} %all-gather.8.cloned.1.call-done) | data formatting | bytes 26214400
  761.3 86.7 %all-gather.4.cloned.1.call-done = bf16[2,1024,3200]{2,1,0:T(8,128)(2,1)} async-done(((bf16[2,32,3200]{2,1,0:T(8,128)(2,1)}), bf16[2,1024,3200]{2,1,0:T(8,128)(2,1)}) %all-gather.4.cloned.1.call-update) | async-done | bytes 13107216 | tf_op jit(solution)/shard_map/all_gather | solution.py:28
  848.1 99.7 %all-gather.6.cloned.1.call-done = bf16[2,1024,3200]{2,1,0:T(8,128)(2,1)} async-done(((bf16[2,32,3200]{2,1,0:T(8,128)(2,1)}), bf16[2,1024,3200]{2,1,0:T(8,128)(2,1)}) %all-gather.6.cloned.1.call-update) | async-done | bytes 13107216 | tf_op jit(solution)/shard_map/all_gather | solution.py:28
  947.7 11.4 %copy.34 = bf16[2,1024,3200]{2,1,0:T(8,128)(2,1)} copy(bf16[2,1024,3200]{2,1,0:T(8,128)(2,1)} %all-gather.4.cloned.1.call-done) | data formatting | bytes 26214400
  959.1 2.0 copy-done
  961.1 4.9 copy.35
  (6 shorter events, 0.0 us)
Async XLA Ops:
  7.2 262.7 %all-reduce.3.cloned.1.call-start = ((), (), s32[]{:S(2)}) async-start(), calls=%async_computation.7 | async-start | bytes 26214400
  31.8 405.0 %reduce-scatter.3.cloned.1.call-start = ((), (), s32[]{:S(2)}) async-start(), calls=%async_computation.2 | async-start | bytes 13516800 | tf_op jit(solution)/shard_map/reduce_scatter | solution.py:22
  31.9 612.1 %copy-start.1 = (f32[2,100,1024]{2,0,1:T(2,128)S(1)}, f32[2,100,1024]{2,0,1:T(2,128)}, u32[]{:S(2)}) copy-start(f32[2,100,1024]{2,0,1:T(2,128)} %param.23) | copy-start | bytes 2457604
  31.9 612.1 %copy-start.2 = (f32[2,100,1024]{2,0,1:T(2,128)S(1)}, f32[2,100,1024]{2,0,1:T(2,128)}, u32[]{:S(2)}) copy-start(f32[2,100,1024]{2,0,1:T(2,128)} %param.20) | copy-start | bytes 2457604
  32.6 616.5 %copy-start.3 = (f32[2,32,3200]{2,1,0:T(8,128)S(1)}, f32[2,32,3200]{2,1,0:T(8,128)}, u32[]{:S(2)}) copy-start(f32[2,32,3200]{2,1,0:T(8,128)} %param.21) | copy-start | bytes 2457604
  32.6 568.9 %reduce-scatter.5.cloned.1.call-start = ((), (), s32[]{:S(2)}) async-start(), calls=%async_computation.3 | async-start | bytes 13516800 | tf_op jit(solution)/shard_map/reduce_scatter | solution.py:22
  33.3 715.0 %all-gather.8.cloned.1.call-start = ((), (), s32[]{:S(2)}) async-start(), calls=%async_computation.6 | async-start | bytes 13516800 | tf_op jit(solution)/shard_map/all_gather | solution.py:28
  649.1 199.0 %all-gather.4.cloned.1.call-start = ((), (), s32[]{:S(2)}) async-start(), calls=%async_computation.4 | async-start | bytes 13516800 | tf_op jit(solution)/shard_map/all_gather | solution.py:28
  652.1 295.7 %all-gather.6.cloned.1.call-start = ((), (), s32[]{:S(2)}) async-start(), calls=%async_computation.5 | async-start | bytes 13516800 | tf_op jit(solution)/shard_map/all_gather | solution.py:28
  947.7 13.4 %copy-start = (bf16[2,1024,3200]{2,1,0:T(8,128)(2,1)S(1)}, bf16[2,1024,3200]{2,1,0:T(8,128)(2,1)}, u32[]{:S(2)}) copy-start(bf16[2,1024,3200]{2,1,0:T(8,128)(2,1)} %all-gather.6.cloned.1.call-done) | copy-start | bytes 39321604
Sparse Core Ops, SparseCore 0:
  31.9 237.8 all-reduce.2
  272.1 164.6 reduce-scatter.2
  439.2 162.2 reduce-scatter.4
  649.2 99.1 all-gather.7
  751.8 96.2 all-gather.3
  851.4 96.2 all-gather.5
where the time goes:
time: 973 us
  waiting for transfers between devices  845 us (87%)
  local copies, waits for them, and re-layouts  57 us (6%)
  blocking collectives  36.9 us (4%)
  other arithmetic  17.2 us (2%)
  between operations  16.8 us (2%)
    reduce_scatter x2, waiting for transfers between devices, step(): lax.psum_scatter(t[0], 'dp', scatter_dimension=1, tiled=True)  327 us
    all_gather x3, waiting for transfers between devices, step(): whole = [lax.all_gather(one[0], 'dp', axis=1, tiled=True) for one in new]  280 us
    unnamed x7, waiting for transfers between devices  238 us
    unnamed x12, local copies, waits for them, and re-layouts  55.9 us
    psum x1, blocking collectives, step(): squares = lax.psum(sum((jnp.sum(g * g) for g in gradients)), 'dp')  36.9 us
  transfers between devices with their start and end apart: 6, of which 6 were waited for; matrix products, arithmetic and copies ran while one was open for 2% of the time, Pallas kernels for 0%

commit v1 on v0

v1 whole, which is shorter than its diff:
```python
import functools
import itertools

import jax
import jax.numpy as jnp
from jax import lax
from jax.experimental import pallas as pl
from jax.experimental.pallas import tpu as pltpu
from jax.sharding import PartitionSpec as P

MESH = pl.DeviceIdType.MESH
F32, BF16 = jnp.float32, jnp.bfloat16

X, Y, Z1, Z0 = range(4)
CHIP_BITS = (16, 8, 4, 2)
ORDERS = ((X, Y, Z0, Z1), (Y, Z0, X, Z1), (Z0, X, Y, Z1))
STEP_OF = {s: 4 - s.bit_length() for s in range(1, 16)}


def adamw(w, m, v, g):
    m = 0.9 * m + 0.1 * g
    v = 0.95 * v + 0.05 * g * g
    step = m * lax.rsqrt(v + 1e-8) + 0.1 * w
    return (w - 0.02 * step).astype(BF16), m, v


class Place:
    def __init__(self):
        me = lax.axis_index("dp")
        self.core = lax.rem(me, 2)
        self.other = 1 - self.core
        self.bits = [lax.rem(lax.div(me, bit), 2) for bit in CHIP_BITS]
        self.partner = [{"dp": me + bit * (1 - 2 * b)} for bit, b in zip(CHIP_BITS, self.bits)]
        self.mate = {"dp": me + 1 - 2 * self.core}

    def block(self, order, slot):
        at = list(self.bits)
        for step, bit in enumerate(order):
            if slot >> (3 - step) & 1:
                at[bit] = 1 - at[bit]
        return tuple(at)

    def greet(self):
        barrier = pltpu.get_barrier_semaphore()
        for device in (*self.partner, self.mate):
            pl.semaphore_signal(barrier, inc=1, device_id=device, device_id_type=MESH)
        pl.semaphore_wait(barrier, 5)


def remote(src, dst, send, recv, device):
    return pltpu.make_async_remote_copy(src_ref=src, dst_ref=dst, send_sem=send, recv_sem=recv, device_id=device, device_id_type=MESH)


def pieces(shape):
    rows, columns = shape
    if rows % 16 == 0:
        return rows // 16, lambda i: (pl.ds(pl.multiple_of(i * 16, 16), 16), slice(None))
    return columns // 128, lambda i: (slice(None), pl.ds(pl.multiple_of(i * 128, 128), 128))


def sum_kernel(*refs):
    n = len(ORDERS)
    refs = iter(refs)
    take = lambda: [next(refs) for _ in range(n)]
    terms, sums, (squares,) = take(), take(), [next(refs)]
    own, mate, got = take(), take(), take()
    partial, own_sem, mate_send, mate_recv, send, recv, out_send, out_recv, sq_send, sq_recv = refs
    here = Place()
    core, other = here.core, here.other
    here.greet()

    def own_copy(w, s):
        at = here.block(ORDERS[w], s)
        return pltpu.make_async_copy(terms[w].at[(core, *at)], own[w].at[s], own_sem.at[w, s])

    def mate_copy(w, s):
        at = here.block(ORDERS[w], s)
        return remote(terms[w].at[(other, *at)], mate[w].at[s], mate_send.at[w, s], mate_recv.at[w, s], here.mate)

    def hop(w, s):
        return remote(own[w].at[s], got[w].at[s], send.at[w, s], recv.at[w, s], here.partner[ORDERS[w][STEP_OF[s]]])

    everything = list(itertools.product(reversed(range(16)), range(n)))
    for s, w in everything:
        mate_copy(w, s).start()
        own_copy(w, s).start()

    squares[...] = jnp.zeros_like(squares)
    for s, w in everything:
        own_copy(w, s).wait()
        mate_copy(w, s).wait_recv()
        arrived = [s + b for b in (8, 4, 2, 1) if s < b]
        for a in arrived:
            hop(w, a).wait_recv()
        count, piece = pieces(own[w].shape[1:])

        def total(i):
            at = (s, *piece(i))
            so_far = own[w][at].astype(F32) + mate[w][at].astype(F32)
            for a in arrived:
                so_far = so_far + got[w][(a, *piece(i))].astype(F32)
            return so_far.astype(BF16)

        if s:

            def body(i, _):
                own[w][(s, *piece(i))] = total(i)
                return _

            lax.fori_loop(0, count, body, 0)
            hop(w, s).start()
        else:

            def body(i, _):
                value = total(i)
                sums[w][(core, *piece(i))] = value
                value = value.astype(F32)
                squares[...] += jnp.sum(value * value)
                return _

            lax.fori_loop(0, count, body, 0)
            remote(sums[w].at[core], sums[w].at[core], out_send.at[w], out_recv.at[w], here.mate).start()

    for i, device in enumerate((here.mate, *here.partner)):
        partial[i] = squares[...]
        copy = remote(partial.at[i], partial.at[5 + i], sq_send.at[i], sq_recv.at[i], device)
        copy.start()
        copy.wait()
        squares[...] += partial[5 + i]

    for w in range(n):
        remote(sums[w].at[other], sums[w].at[other], out_send.at[w], out_recv.at[w], here.mate).wait_recv()
        remote(sums[w].at[core], sums[w].at[core], out_send.at[w], out_recv.at[w], here.mate).wait_send()
    for s, w in everything:
        mate_copy(w, s).wait_send()
        if s:
            hop(w, s).wait_send()


def gather_kernel(*refs):
    n = len(ORDERS)
    refs = iter(refs)
    take = lambda: [next(refs) for _ in range(n)]
    rows, whole, theirs, block = take(), take(), take(), take()
    wide, row_send, row_recv, send, recv, mate_send, mate_recv, own_sem = refs
    here = Place()
    core, other = here.core, here.other
    here.greet()

    def swap(w):
        return remote(rows[w].at[other], theirs[w], row_send.at[w], row_recv.at[w], here.mate)

    def source(w, s):
        return block[w] if s == 0 else whole[w].at[(core, *here.block(ORDERS[w], s))]

    def hop(w, s, step):
        a = s + (8 >> step)
        target = whole[w].at[(core, *here.block(ORDERS[w], s))]
        return remote(source(w, s), target, send.at[w, a], recv.at[w, a], here.partner[ORDERS[w][step]])

    def arrival(w, s):
        target = whole[w].at[(core, *here.block(ORDERS[w], s))]
        return remote(target, target, send.at[w, s], recv.at[w, s], here.partner[ORDERS[w][STEP_OF[s]]])

    def across(w, s):
        target = whole[w].at[(core, *here.block(ORDERS[w], s))]
        return remote(source(w, s), target, mate_send.at[w, s], mate_recv.at[w, s], here.mate)

    def from_across(w, s):
        target = whole[w].at[(other, *here.block(ORDERS[w], s))]
        return remote(target, target, mate_send.at[w, s], mate_recv.at[w, s], here.mate)

    def keep(w):
        return pltpu.make_async_copy(block[w], whole[w].at[(core, *here.bits)], own_sem.at[w])

    for w in range(n):
        swap(w).start()
    for w in range(n):
        swap(w).wait_recv()
        half = rows[w].shape[1]
        mine, his = rows[w][core], theirs[w][...]
        low, high = jnp.where(core == 0, mine, his), jnp.where(core == 0, his, mine)
        if half % 16 == 0:
            block[w][:half] = low
            block[w][half:] = high
        else:
            wide[:half] = low.astype(F32)
            wide[half:] = high.astype(F32)
            block[w][...] = wide[...].astype(BF16)
        for step in reversed(range(4)):
            hop(w, 0, step).start()
        across(w, 0).start()
        keep(w).start()
    for s in range(1, 16):
        for w in range(n):
            arrival(w, s).wait_recv()
            for step in reversed(range(STEP_OF[s])):
                hop(w, s, step).start()
            across(w, s).start()
    for w in range(n):
        swap(w).wait_send()
        keep(w).wait()
        for s in range(16):
            from_across(w, s).wait_recv()
            across(w, s).wait_send()
            for step in range(STEP_OF[s] if s else 4):
                hop(w, s, step).wait_send()


def dma(*shape):
    return pltpu.SemaphoreType.DMA(shape)


def solution(mesh):
    def summed(terms):
        blocks = [t.shape[5:] for t in terms]
        return pl.pallas_call(
            sum_kernel,
            out_shape=[jax.ShapeDtypeStruct((2, *b), BF16) for b in blocks] + [jax.ShapeDtypeStruct((8, 128), F32)],
            in_specs=[pl.BlockSpec(memory_space=pl.ANY)] * 3,
            out_specs=[pl.BlockSpec(memory_space=pltpu.VMEM)] * 4,
            scratch_shapes=[pltpu.VMEM((16, *b), BF16) for b in blocks] * 3
            + [pltpu.VMEM((10, 8, 128), F32)]
            + [dma(3, 16)] * 5
            + [dma(3)] * 2
            + [dma(5)] * 2,
            compiler_params=pltpu.CompilerParams(collective_id=0, has_side_effects=True, vmem_limit_bytes=67_043_328),
            name="sum_terms",
        )(*terms)

    def gathered(rows):
        blocks = [(2 * r.shape[1], r.shape[2]) for r in rows]
        return pl.pallas_call(
            gather_kernel,
            out_shape=[jax.ShapeDtypeStruct((2, 2, 2, 2, 2, *b), BF16) for b in blocks],
            in_specs=[pl.BlockSpec(memory_space=pltpu.VMEM)] * 3,
            out_specs=[pl.BlockSpec(memory_space=pl.ANY)] * 3,
            scratch_shapes=[pltpu.VMEM(r.shape[1:], BF16) for r in rows]
            + [pltpu.VMEM(b, BF16) for b in blocks]
            + [pltpu.VMEM(blocks[2], F32)]
            + [dma(3)] * 2
            + [dma(3, 16)] * 4
            + [dma(3)],
            compiler_params=pltpu.CompilerParams(collective_id=1, has_side_effects=True, vmem_limit_bytes=32 * 2**20),
            name="gather_weights",
        )(*rows)

    def step(*arrays):
        terms, weights, m, v = (arrays[i : i + 3] for i in (0, 3, 6, 9))
        me = lax.axis_index("dp")
        core = lax.rem(me, 2)
        *sums, squares = summed([t[0].reshape(2, 2, 2, 2, 2, -1, t.shape[3]) for t in terms])
        count = sum(w.size for w in weights)
        factor = jnp.minimum(1.0, 0.5 * lax.rsqrt(squares[0, 0] / count + 1e-30))

        def cut(array, index, size):
            return lax.dynamic_slice_in_dim(array, index * size, size, 1).astype(F32)

        new = [adamw(cut(w, me, m.shape[1]), m, v, cut(g, core, m.shape[1]) * factor) for w, m, v, g in zip(weights, m, v, sums, strict=True)]
        whole = [one.reshape(w.shape) for one, w in zip(gathered([one[0] for one in new]), weights, strict=True)]
        return (*whole, *(one[1] for one in new), *(one[2] for one in new))

    all_of, cut_of = P(None, None, None), P(None, "dp", None)
    return jax.shard_map(
        step,
        mesh=mesh,
        in_specs=(P(("rep", "dp"), None, None, None),) * 3 + (all_of,) * 3 + (cut_of,) * 6,
        out_specs=(P("rep", None, None),) * 3 + (P("rep", "dp", None),) * 6,
        check_vma=False,
    )
```

time: 973 us -> 390 us (0.40)
  waiting for transfers between devices: 845 us -> 0 us
  Pallas kernels: 0 us -> 353 us
  blocking collectives: 36.9 us -> 0 us
  local copies, waits for them, and re-layouts: 57 us -> 27.2 us
  between operations: 16.8 us -> 1.4 us
  other arithmetic: 17.2 us -> 7.35 us
    pallas_call x0 -> x2, Pallas kernels: none -> 353 us  [the longest x1 198 us: summed(): pl.pallas_call(sum_kernel, out_shape=[jax.ShapeDtypeStruct((2, *b), BF16)...]
    reduce_scatter x2 -> x0, waiting for transfers between devices: 327 us -> none  [step(): lax.psum_scatter(t[0], 'dp', scatter_dimension=1, tiled=True)]
    all_gather x3 -> x0, waiting for transfers between devices: 280 us -> none  [step(): whole = [lax.all_gather(one[0], 'dp', axis=1, tiled=True) for one in new]]
    unnamed x7 -> x0, waiting for transfers between devices: 238 us -> none
    psum x1 -> x0, blocking collectives: 36.9 us -> none  [step(): squares = lax.psum(sum((jnp.sum(g * g) for g in gradients)), 'dp')]
    unnamed x12 -> x15, local copies, waits for them, and re-layouts: 55.9 us -> 26 us
  transfers between devices with their start and end apart: 6 -> 0, of which waited for: 6 -> 0; matrix products, arithmetic and copies ran while one was open for 2% -> 0% of each run, Pallas kernels for 0% -> 0%
where the time goes in v1:
time: 390 us; the launch traced here: 389 us
  Pallas kernels  353 us (91%)
  local copies, waits for them, and re-layouts  27.2 us (7%)
  other arithmetic  7.35 us (2%)
    pallas_call x1, Pallas kernels, summed(): pl.pallas_call(sum_kernel, out_shape=[jax.ShapeDtypeStruct((2, *b), BF16)...  198 us
    pallas_call x1, Pallas kernels, gathered(): pl.pallas_call(gather_kernel, out_shape=[jax.ShapeDtypeStruct((2, 2, 2, 2...  156 us
    unnamed x15, local copies, waits for them, and re-layouts  26 us

profile of v1, /device:TPU:0, one launch (start us, length us, event | category | flops | bytes accessed | tf_op | source)
XLA Modules:
  0.0 389.4 jit_solution(5073548304034424490)
XLA Ops:
  0.7 197.7 %sum_terms.1 = (bf16[2,64,3200]{2,1,0:T(8,128)(2,1)}, bf16[2,64,3200]{2,1,0:T(8,128)(2,1)}, bf16[2,200,1024]{2,1,0:T(8,128)(2,1)}, f32[8,128]{1,0:T(8,128)}) custom-call(bf16[2,2,2,2,2,64,3200]{6,5,4,3,2,1,0:T(8,128)(2,1)} %bitcast.8, bf16[2,2,2,2,2,64,3200]{6,5,4,3,2,1,0:T(8,128)(2,1)} %bitcast.9, bf16[2,2,2,2,2,200,1024]{6,5,4,3,2,1,0:T(8,128)(2,1)} %bitcast.10), custom_call_target="tpu_custom_call" | custom-call | tf_op jit(solution)/shard_map/sum_terms/pallas_call | solution.py:217
  198.3 1.2 slice.3
  200.2 2.6 fusion.2
  202.8 1.5 copy.24
  204.4 1.5 copy.23
  205.9 4.7 %fusion.7 = (bf16[2,32,3200]{2,1,0:T(8,128)(2,1)S(1)}, f32[2,32,3200]{2,1,0:T(8,128)}, f32[2,32,3200]{2,1,0:T(8,128)}, bf16[2,32,3200]{2,1,0:T(8,128)(2,1)S(1)},...) fusion(bf16[2,1024,3200]{2,1,0:T(8,128)(2,1)} %param.15, s32[]{:T(128)S(6)} %select_n.14, f32[]{:T(128)} %bitcast.3, ...), kind=kLoop, calls=%fused_computation.19 | loop fusion | flops 6963200 | bytes 9011212 | tf_op jit(solution)/shard_map/convert_element_type | solution.py:24
  210.6 155.8 %gather_weights.1 = (bf16[2,2,2,2,2,64,3200]{6,5,4,3,2,1,0:T(8,128)(2,1)S(1)}, bf16[2,2,2,2,2,64,3200]{6,5,4,3,2,1,0:T(8,128)(2,1)}, bf16[2,2,2,2,2,200,1024]{6,5,4,3,2,1,0:T(8,128)(2,1)}) custom-call(bf16[2,32,3200]{2,1,0:T(8,128)(2,1)S(1)} %get-tuple-element.38.refs_0_, bf16[2,32,3200]{2,1,0:T(8,128)(2,1)S(1)} %get-tuple-element.41.refs_1_, ...), custom_call_target="tpu_custom_call" | custom-call | tf_op jit(solution)/shard_map/gather_weights/pallas_call | solution.py:233
  366.4 0.0 copy-start
  366.4 0.0 slice-start
  366.4 0.0 slice-start.1
  366.5 6.6 %copy.36 = bf16[2,1024,3200]{2,1,0:T(8,128)(2,1)} copy(bf16[2,1024,3200]{2,1,0:T(8,128)(2,1)S(1)} %bitcast.7) | data formatting | bytes 26214400
  373.1 2.8 copy-done
  375.9 0.0 slice-start.2
  375.9 0.0 slice-start.3
  375.9 6.6 %copy.37 = bf16[2,1024,3200]{2,1,0:T(8,128)(2,1)} copy(bf16[2,1024,3200]{2,1,0:T(8,128)(2,1)S(1)} %bitcast.14) | data formatting | bytes 26214400
  382.5 0.0 slice-done
  382.5 0.0 slice-done.1
  382.5 1.9 slice-done.2
  384.4 0.0 slice-done.3
  384.5 4.9 %copy.38 = bf16[2,3200,1024]{2,1,0:T(8,128)(2,1)} copy(bf16[2,3200,1024]{2,1,0:T(8,128)(2,1)S(1)} %bitcast.13) | data formatting | bytes 26214400
  (1 shorter events, 0.0 us)
Async XLA Ops:
  366.4 9.5 %copy-start = (bf16[2,2,2,2,2,64,3200]{6,5,4,3,2,1,0:T(8,128)(2,1)S(1)}, bf16[2,2,2,2,2,64,3200]{6,5,4,3,2,1,0:T(8,128)(2,1)}, u32[]{:S(2)}) copy-start(bf16[2,2,2,2,2,64,3200]{6,5,4,3,2,1,0:T(8,128)(2,1)} %get-tuple-element.21) | copy-start | bytes 39321604
  366.4 16.1 %slice-start = ((s8[13107200]{0:T(1024)(128)(4,1)}), s8[4194304]{0:T(1024)(128)(4,1)S(1)}, s32[]{:S(2)}) async-start(s8[13107200]{0:T(1024)(128)(4,1)} %bitcast.11), calls=%async_computation | async-start | bytes 8388608
  366.4 16.1 %slice-start.1 = ((s8[13107200]{0:T(1024)(128)(4,1)}), s8[4194304]{0:T(1024)(128)(4,1)S(1)}, s32[]{:S(2)}) async-start(s8[13107200]{0:T(1024)(128)(4,1)} %bitcast.11), calls=%async_computation.1 | async-start | bytes 8388608
  375.9 8.6 %slice-start.2 = ((s8[13107200]{0:T(1024)(128)(4,1)}), s8[4194304]{0:T(1024)(128)(4,1)S(1)}, s32[]{:S(2)}) async-start(s8[13107200]{0:T(1024)(128)(4,1)} %bitcast.11), calls=%async_computation.2 | async-start | bytes 8388608
  375.9 8.6 %slice-start.3 = ((s8[13107200]{0:T(1024)(128)(4,1)}), s8[524288]{0:T(1024)(128)(4,1)S(1)}, s32[]{:S(2)}) async-start(s8[13107200]{0:T(1024)(128)(4,1)} %bitcast.11), calls=%async_computation.3 | async-start | bytes 1048576

commit v2 on v1

--- a/solution.py
+++ b/solution.py
@@ -13,7 +13,9 @@
 
 X, Y, Z1, Z0 = range(4)
 CHIP_BITS = (16, 8, 4, 2)
-ORDERS = ((X, Y, Z0, Z1), (Y, Z0, X, Z1), (Z0, X, Y, Z1))
+STREAMS = ((0, None, (X, Y, Z0, Z1)), (1, None, (Y, X, Z0, Z1)), (2, 0, (Z0, X, Y, Z1)), (2, 1, (Z0, Y, X, Z1)))
+ORDERS = [order for _, _, order in STREAMS]
+SLOTS = (15, 13, 11, 9, 7, 5, 14, 3, 12, 1, 10, 8, 6, 4, 2, 0)
 STEP_OF = {s: 4 - s.bit_length() for s in range(1, 16)}
 
 
@@ -47,6 +49,15 @@
         pl.semaphore_wait(barrier, 5)
 
 
+def columns(part, shape):
+    half = shape[1] // 2
+    return slice(None) if part is None else pl.ds(part * half, half)
+
+
+def part_shape(part, shape):
+    return shape if part is None else (shape[0], shape[1] // 2)
+
+
 def remote(src, dst, send, recv, device):
     return pltpu.make_async_remote_copy(src_ref=src, dst_ref=dst, send_sem=send, recv_sem=recv, device_id=device, device_id_type=MESH)
 
@@ -59,28 +70,39 @@
 
 
 def sum_kernel(*refs):
-    n = len(ORDERS)
+    n = len(STREAMS)
     refs = iter(refs)
-    take = lambda: [next(refs) for _ in range(n)]
-    terms, sums, (squares,) = take(), take(), [next(refs)]
-    own, mate, got = take(), take(), take()
+    take = lambda count: [next(refs) for _ in range(count)]
+    terms, sums, (squares,) = take(3), take(3), take(1)
+    own, mate, got = take(n), take(n), take(n)
     partial, own_sem, mate_send, mate_recv, send, recv, out_send, out_recv, sq_send, sq_recv = refs
     here = Place()
     core, other = here.core, here.other
     here.greet()
 
+    def term(w, layer, s):
+        which, part, order = STREAMS[w]
+        ref = terms[which]
+        return ref.at[(layer, *here.block(order, s), slice(None), columns(part, ref.shape[5:]))]
+
     def own_copy(w, s):
-        at = here.block(ORDERS[w], s)
-        return pltpu.make_async_copy(terms[w].at[(core, *at)], own[w].at[s], own_sem.at[w, s])
+        return pltpu.make_async_copy(term(w, core, s), own[w].at[s], own_sem.at[w, s])
 
     def mate_copy(w, s):
-        at = here.block(ORDERS[w], s)
-        return remote(terms[w].at[(other, *at)], mate[w].at[s], mate_send.at[w, s], mate_recv.at[w, s], here.mate)
+        return remote(term(w, other, s), mate[w].at[s], mate_send.at[w, s], mate_recv.at[w, s], here.mate)
+
+    def result(w, layer):
+        which, part, _ = STREAMS[w]
+        ref = sums[which].at[layer, :, columns(part, sums[which].shape[1:])]
+        return ref
+
+    def swap(w, layer):
+        return remote(result(w, layer), result(w, layer), out_send.at[w], out_recv.at[w], here.mate)
 
     def hop(w, s):
         return remote(own[w].at[s], got[w].at[s], send.at[w, s], recv.at[w, s], here.partner[ORDERS[w][STEP_OF[s]]])
 
-    everything = list(itertools.product(reversed(range(16)), range(n)))
+    everything = list(itertools.product(SLOTS, range(n)))
     for s, w in everything:
         mate_copy(w, s).start()
         own_copy(w, s).start()
@@ -113,13 +135,14 @@
 
             def body(i, _):
                 value = total(i)
-                sums[w][(core, *piece(i))] = value
+                target = result(w, core)
+                target[piece(i)] = value
                 value = value.astype(F32)
                 squares[...] += jnp.sum(value * value)
                 return _
 
             lax.fori_loop(0, count, body, 0)
-            remote(sums[w].at[core], sums[w].at[core], out_send.at[w], out_recv.at[w], here.mate).start()
+            swap(w, core).start()
 
     for i, device in enumerate((here.mate, *here.partner)):
         partial[i] = squares[...]
@@ -129,8 +152,8 @@
         squares[...] += partial[5 + i]
 
     for w in range(n):
-        remote(sums[w].at[other], sums[w].at[other], out_send.at[w], out_recv.at[w], here.mate).wait_recv()
-        remote(sums[w].at[core], sums[w].at[core], out_send.at[w], out_recv.at[w], here.mate).wait_send()
+        swap(w, other).wait_recv()
+        swap(w, core).wait_send()
     for s, w in everything:
         mate_copy(w, s).wait_send()
         if s:
@@ -138,9 +161,9 @@
 
 
 def gather_kernel(*refs):
-    n = len(ORDERS)
+    n = len(STREAMS)
     refs = iter(refs)
-    take = lambda: [next(refs) for _ in range(n)]
+    take = lambda: [next(refs) for _ in range(3)]
     rows, whole, theirs, block = take(), take(), take(), take()
     wide, row_send, row_recv, send, recv, mate_send, mate_recv, own_sem = refs
     here = Place()
@@ -150,32 +173,36 @@
     def swap(w):
         return remote(rows[w].at[other], theirs[w], row_send.at[w], row_recv.at[w], here.mate)
 
+    def place(w, s, layer):
+        which, part, order = STREAMS[w]
+        ref = whole[which]
+        return ref.at[(layer, *here.block(order, s), slice(None), columns(part, ref.shape[5:]))]
+
     def source(w, s):
-        return block[w] if s == 0 else whole[w].at[(core, *here.block(ORDERS[w], s))]
+        which, part, _ = STREAMS[w]
+        return place(w, s, core) if s else block[which].at[:, columns(part, block[which].shape)]
 
     def hop(w, s, step):
         a = s + (8 >> step)
-        target = whole[w].at[(core, *here.block(ORDERS[w], s))]
-        return remote(source(w, s), target, send.at[w, a], recv.at[w, a], here.partner[ORDERS[w][step]])
+        return remote(source(w, s), place(w, s, core), send.at[w, a], recv.at[w, a], here.partner[ORDERS[w][step]])
 
     def arrival(w, s):
-        target = whole[w].at[(core, *here.block(ORDERS[w], s))]
+        target = place(w, s, core)
         return remote(target, target, send.at[w, s], recv.at[w, s], here.partner[ORDERS[w][STEP_OF[s]]])
 
     def across(w, s):
-        target = whole[w].at[(core, *here.block(ORDERS[w], s))]
-        return remote(source(w, s), target, mate_send.at[w, s], mate_recv.at[w, s], here.mate)
+        return remote(source(w, s), place(w, s, core), mate_send.at[w, s], mate_recv.at[w, s], here.mate)
 
     def from_across(w, s):
-        target = whole[w].at[(other, *here.block(ORDERS[w], s))]
+        target = place(w, s, other)
         return remote(target, target, mate_send.at[w, s], mate_recv.at[w, s], here.mate)
 
     def keep(w):
         return pltpu.make_async_copy(block[w], whole[w].at[(core, *here.bits)], own_sem.at[w])
 
-    for w in range(n):
+    for w in range(3):
         swap(w).start()
-    for w in range(n):
+    for w in range(3):
         swap(w).wait_recv()
         half = rows[w].shape[1]
         mine, his = rows[w][core], theirs[w][...]
@@ -187,19 +214,26 @@
             wide[:half] = low.astype(F32)
             wide[half:] = high.astype(F32)
             block[w][...] = wide[...].astype(BF16)
-        for step in reversed(range(4)):
-            hop(w, 0, step).start()
-        across(w, 0).start()
+        for stream in range(n):
+            if STREAMS[stream][0] == w:
+                for step in (2, 1, 0):
+                    hop(stream, 0, step).start()
+    for stream in range(n):
+        hop(stream, 0, 3).start()
+    for stream in range(n):
+        across(stream, 0).start()
+    for w in range(3):
         keep(w).start()
-    for s in range(1, 16):
+    for s in reversed(SLOTS[:-1]):
         for w in range(n):
             arrival(w, s).wait_recv()
             for step in reversed(range(STEP_OF[s])):
                 hop(w, s, step).start()
             across(w, s).start()
-    for w in range(n):
+    for w in range(3):
         swap(w).wait_send()
         keep(w).wait()
+    for w in range(n):
         for s in range(16):
             from_across(w, s).wait_recv()
             across(w, s).wait_send()
@@ -219,10 +253,10 @@
             out_shape=[jax.ShapeDtypeStruct((2, *b), BF16) for b in blocks] + [jax.ShapeDtypeStruct((8, 128), F32)],
             in_specs=[pl.BlockSpec(memory_space=pl.ANY)] * 3,
             out_specs=[pl.BlockSpec(memory_space=pltpu.VMEM)] * 4,
-            scratch_shapes=[pltpu.VMEM((16, *b), BF16) for b in blocks] * 3
+            scratch_shapes=[pltpu.VMEM((16, *part_shape(part, blocks[which])), BF16) for which, part, _ in STREAMS] * 3
             + [pltpu.VMEM((10, 8, 128), F32)]
-            + [dma(3, 16)] * 5
-            + [dma(3)] * 2
+            + [dma(len(STREAMS), 16)] * 5
+            + [dma(len(STREAMS))] * 2
             + [dma(5)] * 2,
             compiler_params=pltpu.CompilerParams(collective_id=0, has_side_effects=True, vmem_limit_bytes=67_043_328),
             name="sum_terms",
@@ -239,7 +273,7 @@
             + [pltpu.VMEM(b, BF16) for b in blocks]
             + [pltpu.VMEM(blocks[2], F32)]
             + [dma(3)] * 2
-            + [dma(3, 16)] * 4
+            + [dma(len(STREAMS), 16)] * 4
             + [dma(3)],
             compiler_params=pltpu.CompilerParams(collective_id=1, has_side_effects=True, vmem_limit_bytes=32 * 2**20),
             name="gather_weights",

time: 390 us -> 349 us (0.89)
  Pallas kernels: 353 us -> 313 us
    pallas_call x1, Pallas kernels: 198 us -> 162 us  [summed(): pl.pallas_call(sum_kernel, out_shape=[jax.ShapeDtypeStruct((2, *b), BF16)...]
    pallas_call x1, Pallas kernels: 156 us -> 151 us  [gathered(): pl.pallas_call(gather_kernel, out_shape=[jax.ShapeDtypeStruct((2, 2, 2, 2...]
where the time goes in v2:
time: 349 us
  Pallas kernels  313 us (90%)
  local copies, waits for them, and re-layouts  27.2 us (8%)
  other arithmetic  7.35 us (2%)
    pallas_call x1, Pallas kernels, summed(): pl.pallas_call(sum_kernel, out_shape=[jax.ShapeDtypeStruct((2, *b), BF16)...  162 us
    pallas_call x1, Pallas kernels, gathered(): pl.pallas_call(gather_kernel, out_shape=[jax.ShapeDtypeStruct((2, 2, 2, 2...  151 us
    unnamed x15, local copies, waits for them, and re-layouts  26 us
    convert_element_type x2, other arithmetic, adamw(): return ((w - 0.02 * step).astype(BF16), m, v)  7.35 us

profile of v2, /device:TPU:0, one launch (start us, length us, event | category | flops | bytes accessed | tf_op | source)
XLA Modules:
  0.0 349.1 jit_solution(10202349771340393472)
XLA Ops:
  0.7 162.2 %sum_terms.1 = (bf16[2,64,3200]{2,1,0:T(8,128)(2,1)}, bf16[2,64,3200]{2,1,0:T(8,128)(2,1)}, bf16[2,200,1024]{2,1,0:T(8,128)(2,1)}, f32[8,128]{1,0:T(8,128)}) custom-call(bf16[2,2,2,2,2,64,3200]{6,5,4,3,2,1,0:T(8,128)(2,1)} %bitcast.8, bf16[2,2,2,2,2,64,3200]{6,5,4,3,2,1,0:T(8,128)(2,1)} %bitcast.9, bf16[2,2,2,2,2,200,1024]{6,5,4,3,2,1,0:T(8,128)(2,1)} %bitcast.10), custom_call_target="tpu_custom_call" | custom-call | tf_op jit(solution)/shard_map/sum_terms/pallas_call | solution.py:251
  162.9 1.2 slice.3
  164.7 2.6 fusion.2
  167.4 1.5 copy.24
  168.9 1.5 copy.23
  170.4 4.7 %fusion.7 = (bf16[2,32,3200]{2,1,0:T(8,128)(2,1)S(1)}, f32[2,32,3200]{2,1,0:T(8,128)}, f32[2,32,3200]{2,1,0:T(8,128)}, bf16[2,32,3200]{2,1,0:T(8,128)(2,1)S(1)},...) fusion(bf16[2,1024,3200]{2,1,0:T(8,128)(2,1)} %param.15, s32[]{:T(128)S(6)} %select_n.14, f32[]{:T(128)} %bitcast.3, ...), kind=kLoop, calls=%fused_computation.19 | loop fusion | flops 6963200 | bytes 9011212 | tf_op jit(solution)/shard_map/convert_element_type | solution.py:26
  175.1 151.0 %gather_weights.1 = (bf16[2,2,2,2,2,64,3200]{6,5,4,3,2,1,0:T(8,128)(2,1)S(1)}, bf16[2,2,2,2,2,64,3200]{6,5,4,3,2,1,0:T(8,128)(2,1)}, bf16[2,2,2,2,2,200,1024]{6,5,4,3,2,1,0:T(8,128)(2,1)}) custom-call(bf16[2,32,3200]{2,1,0:T(8,128)(2,1)S(1)} %get-tuple-element.38.refs_0_, bf16[2,32,3200]{2,1,0:T(8,128)(2,1)S(1)} %get-tuple-element.41.refs_1_, ...), custom_call_target="tpu_custom_call" | custom-call | tf_op jit(solution)/shard_map/gather_weights/pallas_call | solution.py:267
  326.1 0.0 copy-start
  326.1 0.0 slice-start
  326.1 0.0 slice-start.1
  326.2 6.6 %copy.36 = bf16[2,1024,3200]{2,1,0:T(8,128)(2,1)} copy(bf16[2,1024,3200]{2,1,0:T(8,128)(2,1)S(1)} %bitcast.7) | data formatting | bytes 26214400
  332.8 2.8 copy-done
  335.6 0.0 slice-start.2
  335.6 0.0 slice-start.3
  335.6 6.6 %copy.37 = bf16[2,1024,3200]{2,1,0:T(8,128)(2,1)} copy(bf16[2,1024,3200]{2,1,0:T(8,128)(2,1)S(1)} %bitcast.14) | data formatting | bytes 26214400
  342.2 0.0 slice-done
  342.2 0.0 slice-done.1
  342.2 1.9 slice-done.2
  344.1 0.0 slice-done.3
  344.2 4.9 %copy.38 = bf16[2,3200,1024]{2,1,0:T(8,128)(2,1)} copy(bf16[2,3200,1024]{2,1,0:T(8,128)(2,1)S(1)} %bitcast.13) | data formatting | bytes 26214400
  (1 shorter events, 0.0 us)
Async XLA Ops:
  326.1 9.5 %copy-start = (bf16[2,2,2,2,2,64,3200]{6,5,4,3,2,1,0:T(8,128)(2,1)S(1)}, bf16[2,2,2,2,2,64,3200]{6,5,4,3,2,1,0:T(8,128)(2,1)}, u32[]{:S(2)}) copy-start(bf16[2,2,2,2,2,64,3200]{6,5,4,3,2,1,0:T(8,128)(2,1)} %get-tuple-element.21) | copy-start | bytes 39321604
  326.1 16.1 %slice-start = ((s8[13107200]{0:T(1024)(128)(4,1)}), s8[4194304]{0:T(1024)(128)(4,1)S(1)}, s32[]{:S(2)}) async-start(s8[13107200]{0:T(1024)(128)(4,1)} %bitcast.11), calls=%async_computation | async-start | bytes 8388608
  326.1 16.1 %slice-start.1 = ((s8[13107200]{0:T(1024)(128)(4,1)}), s8[4194304]{0:T(1024)(128)(4,1)S(1)}, s32[]{:S(2)}) async-start(s8[13107200]{0:T(1024)(128)(4,1)} %bitcast.11), calls=%async_computation.1 | async-start | bytes 8388608
  335.6 8.6 %slice-start.2 = ((s8[13107200]{0:T(1024)(128)(4,1)}), s8[4194304]{0:T(1024)(128)(4,1)S(1)}, s32[]{:S(2)}) async-start(s8[13107200]{0:T(1024)(128)(4,1)} %bitcast.11), calls=%async_computation.2 | async-start | bytes 8388608
  335.6 8.6 %slice-start.3 = ((s8[13107200]{0:T(1024)(128)(4,1)}), s8[524288]{0:T(1024)(128)(4,1)S(1)}, s32[]{:S(2)}) async-start(s8[13107200]{0:T(1024)(128)(4,1)} %bitcast.11), calls=%async_computation.3 | async-start | bytes 1048576

commit v3 on v2

--- a/solution.py
+++ b/solution.py
@@ -1,5 +1,4 @@
 import functools
-import itertools
 
 import jax
 import jax.numpy as jnp
@@ -12,10 +11,25 @@
 F32, BF16 = jnp.float32, jnp.bfloat16
 
 X, Y, Z1, Z0 = range(4)
+DEVICES = 32
 CHIP_BITS = (16, 8, 4, 2)
 STREAMS = ((0, None, (X, Y, Z0, Z1)), (1, None, (Y, X, Z0, Z1)), (2, 0, (Z0, X, Y, Z1)), (2, 1, (Z0, Y, X, Z1)))
 ORDERS = [order for _, _, order in STREAMS]
-SLOTS = (15, 13, 11, 9, 7, 5, 14, 3, 12, 1, 10, 8, 6, 4, 2, 0)
+SUM = (
+    (3, 15), (1, 15), (0, 15), (2, 10), (2, 9), (1, 14), (0, 11), (3, 10), (3, 13), (0, 7), (2, 15), (3, 11), (2, 12), (2, 14),
+    (0, 13), (0, 14), (3, 7), (0, 3), (1, 11), (0, 5), (1, 7), (0, 9), (2, 13), (1, 9), (2, 7), (1, 13), (3, 5), (1, 6), (3, 3),
+    (2, 11), (0, 10), (3, 8), (3, 9), (0, 6), (2, 8), (2, 6), (1, 3), (3, 14), (0, 1), (3, 1), (1, 5), (3, 12), (1, 10), (0, 12),
+    (2, 4), (2, 3), (1, 12), (0, 2), (1, 2), (2, 5), (1, 1), (3, 6), (1, 8), (2, 2), (0, 4), (0, 8), (1, 4), (2, 1), (3, 2), (3, 4),
+    (0, 0), (1, 0), (2, 0), (3, 0),
+)
+GATHER = (
+    (3, None, 1), (0, None, 0), (0, None, 2), (1, None, 0), (3, None, 2), (1, None, 2), (0, None, 1), (3, None, 3), (2, None, 3),
+    (2, None, 1), (1, None, 1), (2, None, 2), (3, 1), (0, 2), (2, None, 0), (0, 4), (2, 1), (1, 2), (2, 2), (3, 4), (1, 4),
+    (1, None, 3), (3, 2), (1, 1), (3, 3), (2, 3), (0, 12), (0, None, 3), (1, 6), (1, 10), (0, 6), (2, 10), (3, 5), (1, 3), (0, 1),
+    (2, 7), (0, 10), (3, None, 0), (3, 7), (0, 3), (2, 6), (0, 5), (0, 8), (1, 9), (1, 5), (0, 7), (1, 12), (1, 14), (2, 5), (2, 14),
+    (2, 8), (0, 14), (1, 11), (0, 9), (2, 15), (3, 6), (0, 11), (1, 7), (2, 4), (2, 11), (3, 12), (3, 15), (1, 8), (2, 13), (0, 13),
+    (1, 13), (0, 15), (2, 12), (3, 8), (3, 13), (3, 10), (3, 11), (3, 14), (3, 9), (2, 9), (1, 15),
+)
 STEP_OF = {s: 4 - s.bit_length() for s in range(1, 16)}
 
 
@@ -28,7 +42,7 @@
 
 class Place:
     def __init__(self):
-        me = lax.axis_index("dp")
+        me = self.me = lax.axis_index("dp")
         self.core = lax.rem(me, 2)
         self.other = 1 - self.core
         self.bits = [lax.rem(lax.div(me, bit), 2) for bit in CHIP_BITS]
@@ -42,11 +56,23 @@
                 at[bit] = 1 - at[bit]
         return tuple(at)
 
-    def greet(self):
+    def nth(self, k):
+        return {"dp": lax.rem(self.me + k, DEVICES)}
+
+    def greet(self, everyone=False):
         barrier = pltpu.get_barrier_semaphore()
-        for device in (*self.partner, self.mate):
-            pl.semaphore_signal(barrier, inc=1, device_id=device, device_id_type=MESH)
-        pl.semaphore_wait(barrier, 5)
+        if everyone:
+
+            def signal(k, _):
+                pl.semaphore_signal(barrier, inc=1, device_id=self.nth(k), device_id_type=MESH)
+                return _
+
+            lax.fori_loop(1, DEVICES, signal, 0)
+            pl.semaphore_wait(barrier, DEVICES - 1)
+        else:
+            for device in (*self.partner, self.mate):
+                pl.semaphore_signal(barrier, inc=1, device_id=device, device_id_type=MESH)
+            pl.semaphore_wait(barrier, 5)
 
 
 def columns(part, shape):
@@ -75,10 +101,10 @@
     take = lambda count: [next(refs) for _ in range(count)]
     terms, sums, (squares,) = take(3), take(3), take(1)
     own, mate, got = take(n), take(n), take(n)
-    partial, own_sem, mate_send, mate_recv, send, recv, out_send, out_recv, sq_send, sq_recv = refs
+    parts, own_sem, mate_send, mate_recv, send, recv, out_send, out_recv, sq_send, sq_recv = refs
     here = Place()
     core, other = here.core, here.other
-    here.greet()
+    here.greet(everyone=True)
 
     def term(w, layer, s):
         which, part, order = STREAMS[w]
@@ -102,13 +128,12 @@
     def hop(w, s):
         return remote(own[w].at[s], got[w].at[s], send.at[w, s], recv.at[w, s], here.partner[ORDERS[w][STEP_OF[s]]])
 
-    everything = list(itertools.product(SLOTS, range(n)))
-    for s, w in everything:
+    for w, s in SUM:
         mate_copy(w, s).start()
         own_copy(w, s).start()
 
     squares[...] = jnp.zeros_like(squares)
-    for s, w in everything:
+    for w, s in SUM:
         own_copy(w, s).wait()
         mate_copy(w, s).wait_recv()
         arrived = [s + b for b in (8, 4, 2, 1) if s < b]
@@ -138,23 +163,43 @@
                 target = result(w, core)
                 target[piece(i)] = value
                 value = value.astype(F32)
-                squares[...] += jnp.sum(value * value)
+                value = (value * value).reshape(-1, 8, value.shape[1]).sum(0)
+                squares[...] += sum(value[:, j : j + 128] for j in range(0, value.shape[1], 128))
                 return _
 
             lax.fori_loop(0, count, body, 0)
             swap(w, core).start()
 
-    for i, device in enumerate((here.mate, *here.partner)):
-        partial[i] = squares[...]
-        copy = remote(partial.at[i], partial.at[5 + i], sq_send.at[i], sq_recv.at[i], device)
-        copy.start()
-        copy.wait()
-        squares[...] += partial[5 + i]
-
+    me = here.me
+    parts[me] = squares[...]
+
+    def part_to(k):
+        return remote(parts.at[me], parts.at[me], sq_send.at[k], sq_recv.at[me], here.nth(k))
+
+    def part_from(k):
+        peer = lax.rem(me + k, DEVICES)
+        return remote(parts.at[peer], parts.at[peer], sq_send.at[k], sq_recv.at[peer], here.nth(k))
+
+    def start(k, _):
+        part_to(k).start()
+        return _
+
+    def take_in(k, _):
+        part_from(k).wait_recv()
+        return _
+
+    def drain(k, _):
+        part_to(k).wait_send()
+        return _
+
+    lax.fori_loop(1, DEVICES, start, 0)
+    lax.fori_loop(1, DEVICES, take_in, 0)
+    squares[...] = jnp.full_like(squares, jnp.sum(parts[...]))
+    lax.fori_loop(1, DEVICES, drain, 0)
     for w in range(n):
         swap(w, other).wait_recv()
         swap(w, core).wait_send()
-    for s, w in everything:
+    for w, s in SUM:
         mate_copy(w, s).wait_send()
         if s:
             hop(w, s).wait_send()
@@ -214,22 +259,21 @@
             wide[:half] = low.astype(F32)
             wide[half:] = high.astype(F32)
             block[w][...] = wide[...].astype(BF16)
-        for stream in range(n):
-            if STREAMS[stream][0] == w:
-                for step in (2, 1, 0):
-                    hop(stream, 0, step).start()
-    for stream in range(n):
-        hop(stream, 0, 3).start()
-    for stream in range(n):
-        across(stream, 0).start()
-    for w in range(3):
-        keep(w).start()
-    for s in reversed(SLOTS[:-1]):
-        for w in range(n):
-            arrival(w, s).wait_recv()
-            for step in reversed(range(STEP_OF[s])):
-                hop(w, s, step).start()
-            across(w, s).start()
+    first = True
+    for w, s, *step in GATHER:
+        if step:
+            hop(w, 0, *step).start()
+            continue
+        if first:
+            for stream in range(n):
+                across(stream, 0).start()
+            for weight in range(3):
+                keep(weight).start()
+            first = False
+        arrival(w, s).wait_recv()
+        for step in reversed(range(STEP_OF[s])):
+            hop(w, s, step).start()
+        across(w, s).start()
     for w in range(3):
         swap(w).wait_send()
         keep(w).wait()
@@ -254,10 +298,10 @@
             in_specs=[pl.BlockSpec(memory_space=pl.ANY)] * 3,
             out_specs=[pl.BlockSpec(memory_space=pltpu.VMEM)] * 4,
             scratch_shapes=[pltpu.VMEM((16, *part_shape(part, blocks[which])), BF16) for which, part, _ in STREAMS] * 3
-            + [pltpu.VMEM((10, 8, 128), F32)]
+            + [pltpu.VMEM((DEVICES, 8, 128), F32)]
             + [dma(len(STREAMS), 16)] * 5
             + [dma(len(STREAMS))] * 2
-            + [dma(5)] * 2,
+            + [dma(DEVICES)] * 2,
             compiler_params=pltpu.CompilerParams(collective_id=0, has_side_effects=True, vmem_limit_bytes=67_043_328),
             name="sum_terms",
         )(*terms)
@@ -275,7 +319,7 @@
             + [dma(3)] * 2
             + [dma(len(STREAMS), 16)] * 4
             + [dma(3)],
-            compiler_params=pltpu.CompilerParams(collective_id=1, has_side_effects=True, vmem_limit_bytes=32 * 2**20),
+            compiler_params=pltpu.CompilerParams(collective_id=1, has_side_effects=True, vmem_limit_bytes=10 * 2**20),
             name="gather_weights",
         )(*rows)
 

time: 349 us -> 326 us (0.934)
  Pallas kernels: 313 us -> 298 us
  local copies, waits for them, and re-layouts: 27.2 us -> 19.1 us
    pallas_call x1, Pallas kernels: 162 us -> 153 us  [summed(): pl.pallas_call(sum_kernel, out_shape=[jax.ShapeDtypeStruct((2, *b), BF16)...]
    unnamed x15 -> x5, local copies, waits for them, and re-layouts: 26 us -> 17.9 us
    pallas_call x1, Pallas kernels: 151 us -> 144 us  [gathered(): pl.pallas_call(gather_kernel, out_shape=[jax.ShapeDtypeStruct((2, 2, 2, 2...]
where the time goes in v3:
time: 326 us
  Pallas kernels  298 us (91%)
  local copies, waits for them, and re-layouts  19.1 us (6%)
  other arithmetic  7.35 us (2%)
    pallas_call x1, Pallas kernels, summed(): pl.pallas_call(sum_kernel, out_shape=[jax.ShapeDtypeStruct((2, *b), BF16)...  153 us
    pallas_call x1, Pallas kernels, gathered(): pl.pallas_call(gather_kernel, out_shape=[jax.ShapeDtypeStruct((2, 2, 2, 2...  144 us
    unnamed x5, local copies, waits for them, and re-layouts  17.9 us
    convert_element_type x2, other arithmetic, adamw(): return ((w - 0.02 * step).astype(BF16), m, v)  7.35 us

profile of v3, /device:TPU:0, one launch (start us, length us, event | category | flops | bytes accessed | tf_op | source)
XLA Modules:
  0.0 325.6 jit_solution(10621116528221079342)
XLA Ops:
  0.7 153.3 %sum_terms.1 = (bf16[2,64,3200]{2,1,0:T(8,128)(2,1)}, bf16[2,64,3200]{2,1,0:T(8,128)(2,1)}, bf16[2,200,1024]{2,1,0:T(8,128)(2,1)}, f32[8,128]{1,0:T(8,128)}) custom-call(bf16[2,2,2,2,2,64,3200]{6,5,4,3,2,1,0:T(8,128)(2,1)} %bitcast.10, bf16[2,2,2,2,2,64,3200]{6,5,4,3,2,1,0:T(8,128)(2,1)} %bitcast.11, bf16[2,2,2,2,2,200,1024]{6,5,4,3,2,1,0:T(8,128)(2,1)} %bitcast.12), custom_call_target="tpu_custom_call" | custom-call | tf_op jit(solution)/shard_map/sum_terms/pallas_call | solution.py:295
  154.0 1.2 slice.3
  155.9 2.6 fusion.2
  158.5 1.5 copy.24
  160.0 1.5 copy.23
  161.6 4.7 %fusion.7 = (bf16[2,32,3200]{2,1,0:T(8,128)(2,1)S(1)}, f32[2,32,3200]{2,1,0:T(8,128)}, f32[2,32,3200]{2,1,0:T(8,128)}, bf16[2,32,3200]{2,1,0:T(8,128)(2,1)S(1)},...) fusion(bf16[2,1024,3200]{2,1,0:T(8,128)(2,1)} %param.15, s32[]{:T(128)S(6)} %select_n.14, f32[]{:T(128)} %bitcast.3, ...), kind=kLoop, calls=%fused_computation.19 | loop fusion | flops 6963200 | bytes 9011212 | tf_op jit(solution)/shard_map/convert_element_type | solution.py:40
  166.3 144.5 %gather_weights.1 = (bf16[2,2,2,2,2,64,3200]{6,5,4,3,2,1,0:T(8,128)(2,1)S(1)}, bf16[2,2,2,2,2,64,3200]{6,5,4,3,2,1,0:T(8,128)(2,1)S(1)}, bf16[2,2,2,2,2,200,1024]{6,5,4,3,2,1,0:T(8,128)(2,1)S(1)}) custom-call(bf16[2,32,3200]{2,1,0:T(8,128)(2,1)S(1)} %get-tuple-element.38.refs_0_, bf16[2,32,3200]{2,1,0:T(8,128)(2,1)S(1)} %get-tuple-element.41.refs_1_, ...), custom_call_target="tpu_custom_call" | custom-call | tf_op jit(solution)/shard_map/gather_weights/pallas_call | solution.py:311
  310.8 5.0 %copy.36 = bf16[2,1024,3200]{2,1,0:T(8,128)(2,1)} copy(bf16[2,1024,3200]{2,1,0:T(8,128)(2,1)S(1)} %bitcast.9) | data formatting | bytes 26214400
  315.7 4.9 %copy.37 = bf16[2,1024,3200]{2,1,0:T(8,128)(2,1)} copy(bf16[2,1024,3200]{2,1,0:T(8,128)(2,1)S(1)} %bitcast.8) | data formatting | bytes 26214400
  320.7 4.9 %copy.38 = bf16[2,3200,1024]{2,1,0:T(8,128)(2,1)} copy(bf16[2,3200,1024]{2,1,0:T(8,128)(2,1)S(1)} %bitcast.7) | data formatting | bytes 26214400

commit v4 on v3

--- a/solution.py
+++ b/solution.py
@@ -16,20 +16,16 @@
 STREAMS = ((0, None, (X, Y, Z0, Z1)), (1, None, (Y, X, Z0, Z1)), (2, 0, (Z0, X, Y, Z1)), (2, 1, (Z0, Y, X, Z1)))
 ORDERS = [order for _, _, order in STREAMS]
 SUM = (
-    (3, 15), (1, 15), (0, 15), (2, 10), (2, 9), (1, 14), (0, 11), (3, 10), (3, 13), (0, 7), (2, 15), (3, 11), (2, 12), (2, 14),
-    (0, 13), (0, 14), (3, 7), (0, 3), (1, 11), (0, 5), (1, 7), (0, 9), (2, 13), (1, 9), (2, 7), (1, 13), (3, 5), (1, 6), (3, 3),
-    (2, 11), (0, 10), (3, 8), (3, 9), (0, 6), (2, 8), (2, 6), (1, 3), (3, 14), (0, 1), (3, 1), (1, 5), (3, 12), (1, 10), (0, 12),
-    (2, 4), (2, 3), (1, 12), (0, 2), (1, 2), (2, 5), (1, 1), (3, 6), (1, 8), (2, 2), (0, 4), (0, 8), (1, 4), (2, 1), (3, 2), (3, 4),
-    (0, 0), (1, 0), (2, 0), (3, 0),
+    61, 29, 15, 9, 63, 43, 31, 55, 59, 11, 46, 57, 13, 62, 40, 26, 7, 53, 47, 51, 23, 45, 30, 5, 39, 3, 14, 60, 49, 42, 21, 27, 38, 58,
+    56, 41, 44, 54, 52, 22, 37, 1, 10, 35, 50, 25, 8, 6, 19, 33, 28, 12, 2, 36, 18, 34, 24, 17, 20, 4, 48, 32, 0, 16,
 )
 GATHER = (
-    (3, None, 1), (0, None, 0), (0, None, 2), (1, None, 0), (3, None, 2), (1, None, 2), (0, None, 1), (3, None, 3), (2, None, 3),
-    (2, None, 1), (1, None, 1), (2, None, 2), (3, 1), (0, 2), (2, None, 0), (0, 4), (2, 1), (1, 2), (2, 2), (3, 4), (1, 4),
-    (1, None, 3), (3, 2), (1, 1), (3, 3), (2, 3), (0, 12), (0, None, 3), (1, 6), (1, 10), (0, 6), (2, 10), (3, 5), (1, 3), (0, 1),
-    (2, 7), (0, 10), (3, None, 0), (3, 7), (0, 3), (2, 6), (0, 5), (0, 8), (1, 9), (1, 5), (0, 7), (1, 12), (1, 14), (2, 5), (2, 14),
-    (2, 8), (0, 14), (1, 11), (0, 9), (2, 15), (3, 6), (0, 11), (1, 7), (2, 4), (2, 11), (3, 12), (3, 15), (1, 8), (2, 13), (0, 13),
-    (1, 13), (0, 15), (2, 12), (3, 8), (3, 13), (3, 10), (3, 11), (3, 14), (3, 9), (2, 9), (1, 15),
+    77, 64, 66, 68, 78, 70, 65, 79, 75, 73, 69, 74, 49, 2, 72, 4, 33, 18, 34, 52, 20, 71, 50, 17, 51, 35, 12, 67, 22, 26, 6, 42, 53,
+    19, 1, 39, 10, 76, 55, 3, 38, 5, 8, 25, 21, 7, 28, 30, 37, 46, 40, 14, 27, 9, 47, 54, 11, 23, 36, 43, 60, 63, 24, 45, 13, 29, 15,
+    44, 56, 61, 58, 59, 62, 57, 41, 31,
 )
+SUM = tuple(divmod(entry, 16) for entry in SUM)
+GATHER = tuple(divmod(entry, 16) if entry < 64 else (entry // 4 - 16, None, entry % 4) for entry in GATHER)
 STEP_OF = {s: 4 - s.bit_length() for s in range(1, 16)}
 
 
@@ -59,20 +55,11 @@
     def nth(self, k):
         return {"dp": lax.rem(self.me + k, DEVICES)}
 
-    def greet(self, everyone=False):
+    def greet(self):
         barrier = pltpu.get_barrier_semaphore()
-        if everyone:
-
-            def signal(k, _):
-                pl.semaphore_signal(barrier, inc=1, device_id=self.nth(k), device_id_type=MESH)
-                return _
-
-            lax.fori_loop(1, DEVICES, signal, 0)
-            pl.semaphore_wait(barrier, DEVICES - 1)
-        else:
-            for device in (*self.partner, self.mate):
-                pl.semaphore_signal(barrier, inc=1, device_id=device, device_id_type=MESH)
-            pl.semaphore_wait(barrier, 5)
+        for device in (*self.partner, self.mate):
+            pl.semaphore_signal(barrier, inc=1, device_id=device, device_id_type=MESH)
+        pl.semaphore_wait(barrier, 5)
 
 
 def columns(part, shape):
@@ -100,11 +87,11 @@
     refs = iter(refs)
     take = lambda count: [next(refs) for _ in range(count)]
     terms, sums, (squares,) = take(3), take(3), take(1)
-    own, mate, got = take(n), take(n), take(n)
-    parts, own_sem, mate_send, mate_recv, send, recv, out_send, out_recv, sq_send, sq_recv = refs
+    own, mate, got, final = take(n), take(n), take(n), take(3)
+    parts, own_sem, mate_send, mate_recv, send, recv, out_sem, out_send, out_recv, sq_send, sq_recv = refs
     here = Place()
     core, other = here.core, here.other
-    here.greet(everyone=True)
+    here.greet()
 
     def term(w, layer, s):
         which, part, order = STREAMS[w]
@@ -115,25 +102,38 @@
         return pltpu.make_async_copy(term(w, core, s), own[w].at[s], own_sem.at[w, s])
 
     def mate_copy(w, s):
-        return remote(term(w, other, s), mate[w].at[s], mate_send.at[w, s], mate_recv.at[w, s], here.mate)
-
-    def result(w, layer):
+        return remote(term(w, other, s), mate[w].at[s], mate_send.at[w], mate_recv.at[w, s], here.mate)
+
+    def result(w):
         which, part, _ = STREAMS[w]
-        ref = sums[which].at[layer, :, columns(part, sums[which].shape[1:])]
-        return ref
-
-    def swap(w, layer):
-        return remote(result(w, layer), result(w, layer), out_send.at[w], out_recv.at[w], here.mate)
+        return final[which].at[:, columns(part, final[which].shape)]
+
+    def home(w, layer):
+        which, part, _ = STREAMS[w]
+        return sums[which].at[layer, :, columns(part, final[which].shape)]
+
+    def keep(w):
+        return pltpu.make_async_copy(result(w), home(w, core), out_sem.at[w])
+
+    def swap(w):
+        return remote(result(w), home(w, core), out_send.at[w], out_recv.at[w], here.mate)
+
+    def from_swap(w):
+        return remote(home(w, other), home(w, other), out_send.at[w], out_recv.at[w], here.mate)
 
     def hop(w, s):
-        return remote(own[w].at[s], got[w].at[s], send.at[w, s], recv.at[w, s], here.partner[ORDERS[w][STEP_OF[s]]])
+        return remote(own[w].at[s], got[w].at[s], send.at[w], recv.at[w, s], here.partner[ORDERS[w][STEP_OF[s]]])
 
     for w, s in SUM:
         mate_copy(w, s).start()
         own_copy(w, s).start()
 
     squares[...] = jnp.zeros_like(squares)
-    for w, s in SUM:
+    last = min(SUM.index((w, 0)) for w in range(n))
+    for turn, (w, s) in enumerate(SUM):
+        if turn == last:
+            for stream in range(n):
+                remote(mate[stream], mate[stream], mate_send.at[stream], mate_recv.at[stream, 0], here.mate).wait_send()
         own_copy(w, s).wait()
         mate_copy(w, s).wait_recv()
         arrived = [s + b for b in (8, 4, 2, 1) if s < b]
@@ -160,7 +160,7 @@
 
             def body(i, _):
                 value = total(i)
-                target = result(w, core)
+                target = result(w)
                 target[piece(i)] = value
                 value = value.astype(F32)
                 value = (value * value).reshape(-1, 8, value.shape[1]).sum(0)
@@ -168,41 +168,29 @@
                 return _
 
             lax.fori_loop(0, count, body, 0)
-            swap(w, core).start()
+            keep(w).start()
+            swap(w).start()
 
     me = here.me
     parts[me] = squares[...]
 
     def part_to(k):
-        return remote(parts.at[me], parts.at[me], sq_send.at[k], sq_recv.at[me], here.nth(k))
-
-    def part_from(k):
-        peer = lax.rem(me + k, DEVICES)
-        return remote(parts.at[peer], parts.at[peer], sq_send.at[k], sq_recv.at[peer], here.nth(k))
+        return remote(parts.at[me], parts.at[me], sq_send, sq_recv, here.nth(k))
 
     def start(k, _):
         part_to(k).start()
         return _
 
-    def take_in(k, _):
-        part_from(k).wait_recv()
-        return _
-
-    def drain(k, _):
-        part_to(k).wait_send()
-        return _
-
     lax.fori_loop(1, DEVICES, start, 0)
-    lax.fori_loop(1, DEVICES, take_in, 0)
+    for w in range(n):
+        from_swap(w).wait_recv()
+        keep(w).wait()
+        swap(w).wait_send()
+        sent = own[w].at[pl.ds(1, 15)]
+        remote(sent, sent, send.at[w], recv.at[w, 0], here.mate).wait_send()
+    others = parts.at[pl.ds(0, DEVICES - 1)]
+    remote(others, others, sq_send, sq_recv, here.mate).wait()
     squares[...] = jnp.full_like(squares, jnp.sum(parts[...]))
-    lax.fori_loop(1, DEVICES, drain, 0)
-    for w in range(n):
-        swap(w, other).wait_recv()
-        swap(w, core).wait_send()
-    for w, s in SUM:
-        mate_copy(w, s).wait_send()
-        if s:
-            hop(w, s).wait_send()
 
 
 def gather_kernel(*refs):
@@ -229,18 +217,20 @@
 
     def hop(w, s, step):
         a = s + (8 >> step)
-        return remote(source(w, s), place(w, s, core), send.at[w, a], recv.at[w, a], here.partner[ORDERS[w][step]])
+        return remote(source(w, s), place(w, s, core), send.at[w, step], recv.at[w, a], here.partner[ORDERS[w][step]])
 
     def arrival(w, s):
         target = place(w, s, core)
-        return remote(target, target, send.at[w, s], recv.at[w, s], here.partner[ORDERS[w][STEP_OF[s]]])
+        return remote(target, target, send.at[w, 0], recv.at[w, s], here.partner[ORDERS[w][STEP_OF[s]]])
 
     def across(w, s):
-        return remote(source(w, s), place(w, s, core), mate_send.at[w, s], mate_recv.at[w, s], here.mate)
-
-    def from_across(w, s):
-        target = place(w, s, other)
-        return remote(target, target, mate_send.at[w, s], mate_recv.at[w, s], here.mate)
+        return remote(source(w, s), place(w, s, core), mate_send.at[w], mate_recv.at[w], here.mate)
+
+    def blocks_of(w, layer, *cut):
+        which, part, _ = STREAMS[w]
+        free = (slice(None),) * (5 - len(cut))
+        ref = whole[which].at[(layer, *cut, *free, columns(part, whole[which].shape[5:]))]
+        return remote(ref, ref, mate_send.at[w], mate_recv.at[w], here.mate), ref
 
     def keep(w):
         return pltpu.make_async_copy(block[w], whole[w].at[(core, *here.bits)], own_sem.at[w])
@@ -278,11 +268,25 @@
         swap(w).wait_send()
         keep(w).wait()
     for w in range(n):
-        for s in range(16):
-            from_across(w, s).wait_recv()
-            across(w, s).wait_send()
-            for step in range(STEP_OF[s] if s else 4):
-                hop(w, s, step).wait_send()
+        for step in range(4):
+            _, ref = blocks_of(w, core, *[0] * (step + 1))
+            remote(ref, ref, send.at[w, step], mate_recv.at[w], here.mate).wait_send()
+        blocks_of(w, core)[0].wait_send()
+        blocks_of(w, other)[0].wait_recv()
+
+
+def store_kernel(*refs):
+    held, whole, sem = refs[:3], refs[3:6], refs[6]
+    copies = [
+        pltpu.make_async_copy(a.at[layer, x], b.at[layer, x], sem.at[i, layer, x])
+        for i, (a, b) in enumerate(zip(held, whole))
+        for layer in range(2)
+        for x in range(2)
+    ]
+    for copy in copies:
+        copy.start()
+    for copy in copies:
+        copy.wait()
 
 
 def dma(*shape):
@@ -290,18 +294,21 @@
 
 
 def solution(mesh):
+    n = len(STREAMS)
+
     def summed(terms):
         blocks = [t.shape[5:] for t in terms]
         return pl.pallas_call(
             sum_kernel,
             out_shape=[jax.ShapeDtypeStruct((2, *b), BF16) for b in blocks] + [jax.ShapeDtypeStruct((8, 128), F32)],
             in_specs=[pl.BlockSpec(memory_space=pl.ANY)] * 3,
-            out_specs=[pl.BlockSpec(memory_space=pltpu.VMEM)] * 4,
+            out_specs=[pl.BlockSpec(memory_space=pl.ANY)] * 3 + [pl.BlockSpec(memory_space=pltpu.VMEM)],
             scratch_shapes=[pltpu.VMEM((16, *part_shape(part, blocks[which])), BF16) for which, part, _ in STREAMS] * 3
+            + [pltpu.VMEM(b, BF16) for b in blocks]
             + [pltpu.VMEM((DEVICES, 8, 128), F32)]
-            + [dma(len(STREAMS), 16)] * 5
-            + [dma(len(STREAMS))] * 2
-            + [dma(DEVICES)] * 2,
+            + [dma(n, 16), dma(n), dma(n, 16), dma(n), dma(n, 16)]
+            + [dma(n)] * 3
+            + [dma()] * 2,
             compiler_params=pltpu.CompilerParams(collective_id=0, has_side_effects=True, vmem_limit_bytes=67_043_328),
             name="sum_terms",
         )(*terms)
@@ -317,11 +324,22 @@
             + [pltpu.VMEM(b, BF16) for b in blocks]
             + [pltpu.VMEM(blocks[2], F32)]
             + [dma(3)] * 2
-            + [dma(len(STREAMS), 16)] * 4
+            + [dma(n, 4), dma(n, 16), dma(n), dma(n)]
             + [dma(3)],
             compiler_params=pltpu.CompilerParams(collective_id=1, has_side_effects=True, vmem_limit_bytes=10 * 2**20),
             name="gather_weights",
         )(*rows)
+
+    def stored(held):
+        return pl.pallas_call(
+            store_kernel,
+            out_shape=[jax.ShapeDtypeStruct(h.shape, h.dtype) for h in held],
+            in_specs=[pl.BlockSpec(memory_space=pl.ANY)] * 3,
+            out_specs=[pl.BlockSpec(memory_space=pl.ANY)] * 3,
+            scratch_shapes=[dma(3, 2, 2)],
+            compiler_params=pltpu.CompilerParams(vmem_limit_bytes=2**20),
+            name="store_weights",
+        )(*held)
 
     def step(*arrays):
         terms, weights, m, v = (arrays[i : i + 3] for i in (0, 3, 6, 9))
@@ -335,7 +353,7 @@
             return lax.dynamic_slice_in_dim(array, index * size, size, 1).astype(F32)
 
         new = [adamw(cut(w, me, m.shape[1]), m, v, cut(g, core, m.shape[1]) * factor) for w, m, v, g in zip(weights, m, v, sums, strict=True)]
-        whole = [one.reshape(w.shape) for one, w in zip(gathered([one[0] for one in new]), weights, strict=True)]
+        whole = [one.reshape(w.shape) for one, w in zip(stored(gathered([one[0] for one in new])), weights, strict=True)]
         return (*whole, *(one[1] for one in new), *(one[2] for one in new))
 
     all_of, cut_of = P(None, None, None), P(None, "dp", None)

time: 326 us -> 318 us (0.975)
  local copies, waits for them, and re-layouts: 19.1 us -> 4.23 us
  Pallas kernels: 298 us -> 305 us
    unnamed x5 -> x2, local copies, waits for them, and re-layouts: 17.9 us -> 3.05 us
    pallas_call x0 -> x1, Pallas kernels: none -> 12.8 us  [stored(): pl.pallas_call(store_kernel, out_shape=[jax.ShapeDtypeStruct(h.shape, h.d...]
    pallas_call x1, Pallas kernels: 153 us -> 150 us  [summed(): pl.pallas_call(sum_kernel, out_shape=[jax.ShapeDtypeStruct((2, *b), BF16)...]
where the time goes in v4:
time: 318 us
  Pallas kernels  305 us (96%)
  other arithmetic  7.35 us (2%)
  local copies, waits for them, and re-layouts  4.23 us (1%)
    pallas_call x1, Pallas kernels, summed(): pl.pallas_call(sum_kernel, out_shape=[jax.ShapeDtypeStruct((2, *b), BF16)...  150 us
    pallas_call x1, Pallas kernels, gathered(): pl.pallas_call(gather_kernel, out_shape=[jax.ShapeDtypeStruct((2, 2, 2, 2...  142 us
    pallas_call x1, Pallas kernels, stored(): pl.pallas_call(store_kernel, out_shape=[jax.ShapeDtypeStruct(h.shape, h.d...  12.8 us
    convert_element_type x2, other arithmetic, adamw(): return ((w - 0.02 * step).astype(BF16), m, v)  7.35 us

profile of v4, /device:TPU:0, one launch (start us, length us, event | category | flops | bytes accessed | tf_op | source)
XLA Modules:
  0.0 317.6 jit_solution(8709372052329798963)
XLA Ops:
  0.7 149.8 %sum_terms.1 = (bf16[2,64,3200]{2,1,0:T(8,128)(2,1)}, bf16[2,64,3200]{2,1,0:T(8,128)(2,1)}, bf16[2,200,1024]{2,1,0:T(8,128)(2,1)}, f32[8,128]{1,0:T(8,128)}) custom-call(bf16[2,2,2,2,2,64,3200]{6,5,4,3,2,1,0:T(8,128)(2,1)} %bitcast.7, bf16[2,2,2,2,2,64,3200]{6,5,4,3,2,1,0:T(8,128)(2,1)} %bitcast.8, bf16[2,2,2,2,2,200,1024]{6,5,4,3,2,1,0:T(8,128)(2,1)} %bitcast.9), custom_call_target="tpu_custom_call" | custom-call | tf_op jit(solution)/shard_map/sum_terms/pallas_call | solution.py:301
  150.5 1.2 slice.3
  152.3 2.6 fusion.2
  155.0 1.5 copy.24
  156.5 1.5 copy.23
  158.0 4.7 %fusion.7 = (bf16[2,32,3200]{2,1,0:T(8,128)(2,1)S(1)}, f32[2,32,3200]{2,1,0:T(8,128)}, f32[2,32,3200]{2,1,0:T(8,128)}, bf16[2,32,3200]{2,1,0:T(8,128)(2,1)S(1)},...) fusion(bf16[2,1024,3200]{2,1,0:T(8,128)(2,1)} %param.15, s32[]{:T(128)S(6)} %select_n.14, f32[]{:T(128)} %bitcast.3, ...), kind=kLoop, calls=%fused_computation.19 | loop fusion | flops 6963200 | bytes 9011212 | tf_op jit(solution)/shard_map/convert_element_type | solution.py:36
  162.8 142.0 %gather_weights.1 = (bf16[2,2,2,2,2,64,3200]{6,5,4,3,2,1,0:T(8,128)(2,1)S(1)}, bf16[2,2,2,2,2,64,3200]{6,5,4,3,2,1,0:T(8,128)(2,1)S(1)}, bf16[2,2,2,2,2,200,1024]{6,5,4,3,2,1,0:T(8,128)(2,1)S(1)}) custom-call(bf16[2,32,3200]{2,1,0:T(8,128)(2,1)S(1)} %get-tuple-element.44.refs_0_, bf16[2,32,3200]{2,1,0:T(8,128)(2,1)S(1)} %get-tuple-element.47.refs_1_, ...), custom_call_target="tpu_custom_call" | custom-call | tf_op jit(solution)/shard_map/gather_weights/pallas_call | solution.py:318
  304.8 12.8 %store_weights.1 = (bf16[2,2,2,2,2,64,3200]{6,5,4,3,2,1,0:T(8,128)(2,1)}, bf16[2,2,2,2,2,64,3200]{6,5,4,3,2,1,0:T(8,128)(2,1)}, bf16[2,2,2,2,2,200,1024]{6,5,4,3,2,1,0:T(8,128)(2,1)}) custom-call(bf16[2,2,2,2,2,64,3200]{6,5,4,3,2,1,0:T(8,128)(2,1)S(1)} %get-tuple-element.23.refs_0_, bf16[2,2,2,2,2,64,3200]{6,5,4,3,2,1,0:T(8,128)(2,1)S(1)} %get-tuple-element.24.refs_1_, ...), custom_call_target="tpu_custom_call" | custom-call | tf_op jit(solution)/shard_map/store_weights/pallas_call | solution.py:334

commit v5 on v4

--- a/solution.py
+++ b/solution.py
@@ -36,6 +36,9 @@
     return (w - 0.02 * step).astype(BF16), m, v
 
 
+STORE_REFS = ((0, 3), (3, 2), (5, 3), (8, 2), (10, 2), (12, 2), (14, 1), (15, 1), (16, 1))
+
+
 class Place:
     def __init__(self):
         me = self.me = lax.axis_index("dp")
@@ -91,8 +94,6 @@
     parts, own_sem, mate_send, mate_recv, send, recv, out_sem, out_send, out_recv, sq_send, sq_recv = refs
     here = Place()
     core, other = here.core, here.other
-    here.greet()
-
     def term(w, layer, s):
         which, part, order = STREAMS[w]
         ref = terms[which]
@@ -124,8 +125,12 @@
     def hop(w, s):
         return remote(own[w].at[s], got[w].at[s], send.at[w], recv.at[w, s], here.partner[ORDERS[w][STEP_OF[s]]])
 
+    for w, s in SUM[:16]:
+        own_copy(w, s).start()
+    here.greet()
     for w, s in SUM:
         mate_copy(w, s).start()
+    for w, s in SUM[16:]:
         own_copy(w, s).start()
 
     squares[...] = jnp.zeros_like(squares)
@@ -276,16 +281,24 @@
 
 
 def store_kernel(*refs):
-    held, whole, sem = refs[:3], refs[3:6], refs[6]
+    held, moments, whole, turned, flat, middle, sem, in_sem, out_sem = (refs[i : i + n] for i, n in STORE_REFS)
+    (sem,), (in_sem,), (out_sem,) = sem, in_sem, out_sem
     copies = [
         pltpu.make_async_copy(a.at[layer, x], b.at[layer, x], sem.at[i, layer, x])
         for i, (a, b) in enumerate(zip(held, whole))
         for layer in range(2)
         for x in range(2)
     ]
-    for copy in copies:
+    inward = [pltpu.make_async_copy(a, b, in_sem.at[i]) for i, (a, b) in enumerate(zip(moments, flat))]
+    outward = [pltpu.make_async_copy(a, b, out_sem.at[i]) for i, (a, b) in enumerate(zip(middle, turned))]
+    for copy in (*inward, *copies):
         copy.start()
-    for copy in copies:
+    for i in range(2):
+        inward[i].wait()
+        for layer in range(2):
+            middle[i][:, layer, :] = flat[i][layer]
+        outward[i].start()
+    for copy in (*copies, *outward):
         copy.wait()
 
 
@@ -330,16 +343,17 @@
             name="gather_weights",
         )(*rows)
 
-    def stored(held):
+    def stored(held, moments):
+        turned = [jax.ShapeDtypeStruct((m.shape[1], m.shape[0], m.shape[2]), F32) for m in moments]
         return pl.pallas_call(
             store_kernel,
-            out_shape=[jax.ShapeDtypeStruct(h.shape, h.dtype) for h in held],
-            in_specs=[pl.BlockSpec(memory_space=pl.ANY)] * 3,
-            out_specs=[pl.BlockSpec(memory_space=pl.ANY)] * 3,
-            scratch_shapes=[dma(3, 2, 2)],
-            compiler_params=pltpu.CompilerParams(vmem_limit_bytes=2**20),
+            out_shape=[jax.ShapeDtypeStruct(h.shape, h.dtype) for h in held] + turned,
+            in_specs=[pl.BlockSpec(memory_space=pl.ANY)] * 5,
+            out_specs=[pl.BlockSpec(memory_space=pl.ANY)] * 5,
+            scratch_shapes=[pltpu.VMEM(m.shape, F32) for m in moments] + [pltpu.VMEM(t.shape, F32) for t in turned] + [dma(3, 2, 2), dma(2), dma(2)],
+            compiler_params=pltpu.CompilerParams(vmem_limit_bytes=6 * 2**20),
             name="store_weights",
-        )(*held)
+        )(*held, *moments)
 
     def step(*arrays):
         terms, weights, m, v = (arrays[i : i + 3] for i in (0, 3, 6, 9))
@@ -353,8 +367,10 @@
             return lax.dynamic_slice_in_dim(array, index * size, size, 1).astype(F32)
 
         new = [adamw(cut(w, me, m.shape[1]), m, v, cut(g, core, m.shape[1]) * factor) for w, m, v, g in zip(weights, m, v, sums, strict=True)]
-        whole = [one.reshape(w.shape) for one, w in zip(stored(gathered([one[0] for one in new])), weights, strict=True)]
-        return (*whole, *(one[1] for one in new), *(one[2] for one in new))
+        *held, m_down, v_down = stored(gathered([one[0] for one in new]), new[2][1:])
+        whole = [one.reshape(w.shape) for one, w in zip(held, weights, strict=True)]
+        m_down, v_down = (jnp.transpose(one, (1, 0, 2)) for one in (m_down, v_down))
+        return (*whole, new[0][1], new[1][1], m_down, new[0][2], new[1][2], v_down)
 
     all_of, cut_of = P(None, None, None), P(None, "dp", None)
     return jax.shard_map(

time: 318 us -> 316 us (level)
  no operation moved by 1% of the time
where the time goes in v5:
time: 316 us; the launch traced here: 315 us
  Pallas kernels  305 us (97%)
  other arithmetic  7.37 us (2%)
    pallas_call x1, Pallas kernels, summed(): pl.pallas_call(sum_kernel, out_shape=[jax.ShapeDtypeStruct((2, *b), BF16)...  150 us
    pallas_call x1, Pallas kernels, gathered(): pl.pallas_call(gather_kernel, out_shape=[jax.ShapeDtypeStruct((2, 2, 2, 2...  142 us
    pallas_call x1, Pallas kernels, stored(): pl.pallas_call(store_kernel, out_shape=[jax.ShapeDtypeStruct(h.shape, h.d...  13.6 us
    convert_element_type x2, other arithmetic, adamw(): return ((w - 0.02 * step).astype(BF16), m, v)  7.37 us

profile of v5, /device:TPU:0, one launch (start us, length us, event | category | flops | bytes accessed | tf_op | source)
XLA Modules:
  0.0 315.4 jit_solution(1960233738039646461)
XLA Ops:
  0.7 149.5 %sum_terms.1 = (bf16[2,64,3200]{2,1,0:T(8,128)(2,1)}, bf16[2,64,3200]{2,1,0:T(8,128)(2,1)}, bf16[2,200,1024]{2,1,0:T(8,128)(2,1)}, f32[8,128]{1,0:T(8,128)}) custom-call(bf16[2,2,2,2,2,64,3200]{6,5,4,3,2,1,0:T(8,128)(2,1)} %bitcast.9, bf16[2,2,2,2,2,64,3200]{6,5,4,3,2,1,0:T(8,128)(2,1)} %bitcast.10, bf16[2,2,2,2,2,200,1024]{6,5,4,3,2,1,0:T(8,128)(2,1)} %bitcast.11), custom_call_target="tpu_custom_call" | custom-call | tf_op jit(solution)/shard_map/sum_terms/pallas_call | solution.py:314
  150.2 1.2 slice.3
  152.1 2.6 fusion.2
  154.7 4.7 %fusion.7 = (bf16[2,32,3200]{2,1,0:T(8,128)(2,1)S(1)}, f32[2,32,3200]{2,1,0:T(8,128)}, f32[2,32,3200]{2,1,0:T(8,128)}, bf16[2,32,3200]{2,1,0:T(8,128)(2,1)S(1)},...) fusion(bf16[2,1024,3200]{2,1,0:T(8,128)(2,1)} %param.15, s32[]{:T(128)S(6)} %select_n.14, f32[]{:T(128)} %bitcast.3, ...), kind=kLoop, calls=%fused_computation.19 | loop fusion | flops 6963200 | bytes 9011212 | tf_op jit(solution)/shard_map/convert_element_type | solution.py:36
  159.4 142.4 %gather_weights.1 = (bf16[2,2,2,2,2,64,3200]{6,5,4,3,2,1,0:T(8,128)(2,1)S(1)}, bf16[2,2,2,2,2,64,3200]{6,5,4,3,2,1,0:T(8,128)(2,1)S(1)}, bf16[2,2,2,2,2,200,1024]{6,5,4,3,2,1,0:T(8,128)(2,1)S(1)}) custom-call(bf16[2,32,3200]{2,1,0:T(8,128)(2,1)S(1)} %get-tuple-element.39.refs_0_, bf16[2,32,3200]{2,1,0:T(8,128)(2,1)S(1)} %get-tuple-element.42.refs_1_, ...), custom_call_target="tpu_custom_call" | custom-call | tf_op jit(solution)/shard_map/gather_weights/pallas_call | solution.py:331
  301.9 13.6 %store_weights.1 = (bf16[2,2,2,2,2,64,3200]{6,5,4,3,2,1,0:T(8,128)(2,1)}, bf16[2,2,2,2,2,64,3200]{6,5,4,3,2,1,0:T(8,128)(2,1)}, bf16[2,2,2,2,2,200,1024]{6,5,4,3...) custom-call(bf16[2,2,2,2,2,64,3200]{6,5,4,3,2,1,0:T(8,128)(2,1)S(1)} %get-tuple-element.25.refs_0_, ...), custom_call_target="tpu_custom_call" | custom-call | tf_op jit(solution)/shard_map/store_weights/pallas_call | solution.py:348

commit v6 on v5

--- a/solution.py
+++ b/solution.py
@@ -38,6 +38,8 @@
 
 STORE_REFS = ((0, 3), (3, 2), (5, 3), (8, 2), (10, 2), (12, 2), (14, 1), (15, 1), (16, 1))
 
+EARLY = next(i for i, entry in enumerate(GATHER) if len(entry) == 2)
+
 
 class Place:
     def __init__(self):
@@ -254,8 +256,11 @@
             wide[:half] = low.astype(F32)
             wide[half:] = high.astype(F32)
             block[w][...] = wide[...].astype(BF16)
+        for stream, _, *step in GATHER[:EARLY]:
+            if STREAMS[stream][0] == w:
+                hop(stream, 0, *step).start()
     first = True
-    for w, s, *step in GATHER:
+    for w, s, *step in GATHER[EARLY:]:
         if step:
             hop(w, 0, *step).start()
             continue

time: 316 us -> 315 us (level)
  no operation moved by 1% of the time
where the time goes in v6:
time: 315 us
  Pallas kernels  305 us (97%)
  other arithmetic  7.37 us (2%)
    pallas_call x1, Pallas kernels, summed(): pl.pallas_call(sum_kernel, out_shape=[jax.ShapeDtypeStruct((2, *b), BF16)...  150 us
    pallas_call x1, Pallas kernels, gathered(): pl.pallas_call(gather_kernel, out_shape=[jax.ShapeDtypeStruct((2, 2, 2, 2...  142 us
    pallas_call x1, Pallas kernels, stored(): pl.pallas_call(store_kernel, out_shape=[jax.ShapeDtypeStruct(h.shape, h.d...  13.6 us
    convert_element_type x2, other arithmetic, adamw(): return ((w - 0.02 * step).astype(BF16), m, v)  7.37 us

profile of v6, /device:TPU:0, one launch (start us, length us, event | category | flops | bytes accessed | tf_op | source)
XLA Modules:
  0.0 314.7 jit_solution(15408577690944132289)
XLA Ops:
  0.7 149.5 %sum_terms.1 = (bf16[2,64,3200]{2,1,0:T(8,128)(2,1)}, bf16[2,64,3200]{2,1,0:T(8,128)(2,1)}, bf16[2,200,1024]{2,1,0:T(8,128)(2,1)}, f32[8,128]{1,0:T(8,128)}) custom-call(bf16[2,2,2,2,2,64,3200]{6,5,4,3,2,1,0:T(8,128)(2,1)} %bitcast.9, bf16[2,2,2,2,2,64,3200]{6,5,4,3,2,1,0:T(8,128)(2,1)} %bitcast.10, bf16[2,2,2,2,2,200,1024]{6,5,4,3,2,1,0:T(8,128)(2,1)} %bitcast.11), custom_call_target="tpu_custom_call" | custom-call | tf_op jit(solution)/shard_map/sum_terms/pallas_call | solution.py:319
  150.2 1.2 slice.3
  152.1 2.6 fusion.2
  154.7 4.7 %fusion.7 = (bf16[2,32,3200]{2,1,0:T(8,128)(2,1)S(1)}, f32[2,32,3200]{2,1,0:T(8,128)}, f32[2,32,3200]{2,1,0:T(8,128)}, bf16[2,32,3200]{2,1,0:T(8,128)(2,1)S(1)},...) fusion(bf16[2,1024,3200]{2,1,0:T(8,128)(2,1)} %param.15, s32[]{:T(128)S(6)} %select_n.14, f32[]{:T(128)} %bitcast.3, ...), kind=kLoop, calls=%fused_computation.19 | loop fusion | flops 6963200 | bytes 9011212 | tf_op jit(solution)/shard_map/convert_element_type | solution.py:36
  159.4 141.7 %gather_weights.1 = (bf16[2,2,2,2,2,64,3200]{6,5,4,3,2,1,0:T(8,128)(2,1)S(1)}, bf16[2,2,2,2,2,64,3200]{6,5,4,3,2,1,0:T(8,128)(2,1)S(1)}, bf16[2,2,2,2,2,200,1024]{6,5,4,3,2,1,0:T(8,128)(2,1)S(1)}) custom-call(bf16[2,32,3200]{2,1,0:T(8,128)(2,1)S(1)} %get-tuple-element.39.refs_0_, bf16[2,32,3200]{2,1,0:T(8,128)(2,1)S(1)} %get-tuple-element.42.refs_1_, ...), custom_call_target="tpu_custom_call" | custom-call | tf_op jit(solution)/shard_map/gather_weights/pallas_call | solution.py:336
  301.1 13.6 %store_weights.1 = (bf16[2,2,2,2,2,64,3200]{6,5,4,3,2,1,0:T(8,128)(2,1)}, bf16[2,2,2,2,2,64,3200]{6,5,4,3,2,1,0:T(8,128)(2,1)}, bf16[2,2,2,2,2,200,1024]{6,5,4,3...) custom-call(bf16[2,2,2,2,2,64,3200]{6,5,4,3,2,1,0:T(8,128)(2,1)S(1)} %get-tuple-element.25.refs_0_, ...), custom_call_target="tpu_custom_call" | custom-call | tf_op jit(solution)/shard_map/store_weights/pallas_call | solution.py:353
